TPU v7x, 32 devices: a whole 2x2x4 slice. The times are simulated.
32 devices in a mesh: groups: 2 (over y), mp: 2 (over x), expert: 4 (over z), dp: 2 (over core).
Axes of the slice: x: 2, y: 2, z: 4, core: 2. Of those that a mesh axis runs over, the one named last changes fastest.
Arguments:
- hidden_in: bfloat16 [1024, 4096], P(('groups', 'expert', 'dp'), 'mp'), parts along dimension 0, may hold values from -6 to 6
- norm_gain: bfloat16 [2, 4096], P(None, 'mp'), may hold values from 0.25 to 1.75
- expert_ids: int32 [2, 1024, 2], P(None, ('groups', 'expert', 'dp')), parts along dimension 1, may hold values from 0 to 3, all different within a row; in each aligned block of 64 rows (0 to 63, 64 to 127, ..., all dimensions but the last counted through in order) at most 64 rows name the same one
- gate_counts: int32 [2, 1024, 2], P(None, ('groups', 'expert', 'dp')), parts along dimension 1, may hold values from 8 to 15
- exit_layer: int32 [1024], P(('groups', 'expert', 'dp')), parts along dimension 0, may hold values from 1 to 2
- w_gate: bfloat16 [2, 4, 7168, 4096], P(None, 'expert', ('mp', 'dp')), may hold values from -0.09375 to 0.09375
- w_up: bfloat16 [2, 4, 7168, 4096], P(None, 'expert', ('mp', 'dp')), may hold values from -0.09375 to 0.09375
- w_down: bfloat16 [2, 4, 7168, 4096], P(None, 'expert', ('mp', 'dp')), may hold values from -0.0625 to 0.0625
Outputs:
- hidden_out: bfloat16 [1024, 4096], P(('groups', 'expert', 'dp'), 'mp'), parts along dimension 0
There are 2 independent parts, one for each index of `groups`. A program takes and returns all parts, laid end to end along the dimension named above; an argument that names none is the same for every part. Nothing has to cross between parts.
Inputs may be any that keep to these rules, and one draw needn't show every extreme that they name: `expert_ids`: A token's two ids in a layer differ. In the rows of one device in one layer (aligned blocks of 64 rows, layer by layer) some expert may be named by all 64 rows.
All inputs are finite; a program needn't handle non-finite values.
Results may differ from a plain program's by a relative error of at most 0.014.
Values may be sent and summed in bfloat16 or wider, within the bound.
A program may use at most 384 MiB of HBM per device.

v0:
```python
import jax
import jax.numpy as jnp
from jax import lax
from jax.sharding import PartitionSpec as P

LAYERS = 2


norm_floor = 0.1


def body(hidden_in, norm_gain, expert_ids, gate_counts, exit_layer, w_gate, w_up, w_down):
    experts = lax.axis_size("expert")
    shards = lax.axis_size("mp")
    tok_rows, slice_width = hidden_in.shape
    full_width = slice_width * shards
    contract = (((1,), (1,)), ((), ()))
    expert_range = jnp.arange(experts, dtype=jnp.int32)
    slot_range = jnp.arange(tok_rows, dtype=jnp.int32)
    current = hidden_in
    for layer_idx in range(LAYERS):
        counts = gate_counts[layer_idx].astype(jnp.float32)
        gate_share = counts / jnp.sum(counts, axis=1, keepdims=True)
        active = exit_layer > layer_idx
        matched = (expert_ids[layer_idx][:, :, None] == expert_range[None, None, :]) & active[
            :, None, None
        ]
        chosen = jnp.sum(matched.astype(jnp.int32), axis=1)
        weight_te = jnp.sum(jnp.where(matched, gate_share[:, :, None], jnp.float32(0.0)), axis=1)
        slot_rank = jnp.cumsum(chosen, axis=0) - chosen
        place_mask = (slot_rank.T[:, None, :] == slot_range[None, :, None]) & (
            chosen.T[:, None, :] > 0
        )
        place_bf = place_mask.astype(jnp.bfloat16)
        current_f32 = current.astype(jnp.float32)
        whole_rows, whole_gain = (
            lax.all_gather(current, "mp", axis=1, tiled=True),
            lax.all_gather(norm_gain[layer_idx], "mp", axis=0, tiled=True),
        )
        whole_f32 = whole_rows.astype(jnp.float32)
        sum_squares = jnp.sum(whole_f32 * whole_f32, axis=1)
        inv_rms = lax.rsqrt(sum_squares / full_width + norm_floor)
        normed = (whole_f32 * inv_rms[:, None] * whole_gain.astype(jnp.float32)[None, :]).astype(
            jnp.bfloat16
        )
        outgoing = jnp.einsum(
            "ect,td->ecd", place_bf, normed, preferred_element_type=jnp.float32
        ).astype(jnp.bfloat16)
        incoming = lax.all_to_all(outgoing, "expert", split_axis=0, concat_axis=0, tiled=True)
        inputs = incoming.reshape(experts * tok_rows, full_width)
        gate_rows = lax.all_gather(w_gate[layer_idx, 0], "dp", axis=0, tiled=True)
        up_rows = lax.all_gather(w_up[layer_idx, 0], "dp", axis=0, tiled=True)
        down_rows = lax.all_gather(w_down[layer_idx, 0], "dp", axis=0, tiled=True)
        gate_val = lax.dot_general(inputs, gate_rows, contract, preferred_element_type=jnp.float32)
        up_val = lax.dot_general(inputs, up_rows, contract, preferred_element_type=jnp.float32)
        hidden = (jax.nn.silu(gate_val) * up_val).astype(jnp.bfloat16)
        partial_value = jnp.dot(hidden, down_rows, preferred_element_type=jnp.float32)
        summed = lax.psum_scatter(
            partial_value.astype(jnp.bfloat16), "mp", scatter_dimension=1, tiled=True
        )
        returned = lax.all_to_all(
            summed.reshape(experts, tok_rows, slice_width),
            "expert",
            split_axis=0,
            concat_axis=0,
            tiled=True,
        )
        place_weight = place_mask.astype(jnp.float32) * weight_te.T[:, None, :]
        update = jnp.einsum(
            "ect,ecd->td",
            place_weight,
            returned.astype(jnp.float32),
            precision=lax.Precision.HIGHEST,
        )
        current = (current_f32 + update).astype(jnp.bfloat16)
    return current


def solution(mesh):
    in_specs = (
        P(("groups", "expert", "dp"), "mp"),
        P(None, "mp"),
        P(None, ("groups", "expert", "dp"), None),
        P(None, ("groups", "expert", "dp"), None),
        P(("groups", "expert", "dp")),
        P(None, "expert", ("mp", "dp"), None),
        P(None, "expert", ("mp", "dp"), None),
        P(None, "expert", ("mp", "dp"), None),
    )
    out_specs = P(("groups", "expert", "dp"), "mp")
    return jax.shard_map(body, mesh=mesh, in_specs=in_specs, out_specs=out_specs, check_vma=False)
```

profile of v0, /device:TPU:0, one launch (start us, length us, event | category | flops | bytes accessed | tf_op | source)
XLA Modules:
  0.0 487.9 jit_solution(12572547919822806990)
XLA Ops:
  6.5 0.0 all-gather.15.cloned.1.call-start
  6.5 22.0 %fusion.78 = (bf16[1,1,1792,4096]{3,2,1,0:T(8,128)(2,1)}, bf16[1,1,1792,4096]{3,2,1,0:T(8,128)(2,1)}) fusion(bf16[2,1,1792,4096]{3,2,1,0:T(8,128)(2,1)} %param.13), kind=kLoop, calls=%fused_computation.86 | loop fusion | bytes 58720256 | tf_op jit(solution)/shard_map/slice | solution.py:51
  28.5 0.0 all-gather.15.cloned.1.call-update
  28.5 0.0 all-gather.17.cloned.1.call-start
  28.6 25.5 %fusion.79 = (bf16[1,1,1792,4096]{3,2,1,0:T(8,128)(2,1)}, bf16[1,1,1792,4096]{3,2,1,0:T(8,128)(2,1)}) fusion(bf16[2,1,1792,4096]{3,2,1,0:T(8,128)(2,1)} %param.14), kind=kLoop, calls=%fused_computation.87 | loop fusion | bytes 58720256 | tf_op jit(solution)/shard_map/slice | solution.py:52
  54.1 0.0 all-gather.17.cloned.1.call-update
  54.1 0.0 all-gather.19.cloned.1.call-start
  54.2 22.4 %fusion.80 = (bf16[1,1,1792,4096]{3,2,1,0:T(8,128)(2,1)}, bf16[1,1,1792,4096]{3,2,1,0:T(8,128)(2,1)}) fusion(bf16[2,1,1792,4096]{3,2,1,0:T(8,128)(2,1)} %param.15), kind=kLoop, calls=%fused_computation.88 | loop fusion | bytes 58720256 | tf_op jit(solution)/shard_map/slice | solution.py:53
  76.6 0.0 copy-start.4
  76.6 0.0 copy-start.3
  76.6 0.0 copy-start.1
  76.6 0.0 copy-start
  76.6 0.0 all-gather.19.cloned.1.call-update
  76.6 0.0 reduce-scatter.3.cloned.1.call-start
  76.7 0.6 copy-done.4
  77.2 0.0 copy-done.3
  77.3 0.1 copy.19
  77.4 0.1 reduce_window_sum.17
  77.5 0.1 copy.21
  77.6 0.0 copy-done.1
  77.6 7.8 %all-gather = bf16[1,4096]{1,0:T(2,128)(2,1)S(1)} all-gather(bf16[1,2048]{1,0:T(2,128)(2,1)S(1)} %get-tuple-element.14), channel_id=2, replica_groups=mesh['groups'=2,'mp'=2,'expert'=4,'dp'=2] {'mp'}, dimensions={1}, use_global_device_ids=true | all-gather | bytes 12288 | tf_op jit(solution)/shard_map/all_gather | solution.py:38
  85.4 0.0 copy-done
  85.4 7.1 %all_gather.30 = bf16[64,4096]{1,0:T(8,128)(2,1)S(1)} all-gather(bf16[64,2048]{1,0:T(8,128)(2,1)S(1)} %copy-done), channel_id=1, replica_groups=mesh['groups'=2,'mp'=2,'expert'=4,'dp'=2] {'mp'}, dimensions={1}, use_global_device_ids=true | all-gather | bytes 786432 | tf_op jit(solution)/shard_map/all_gather | solution.py:37
  92.5 0.2 fusion.38
  92.7 0.9 convolution_convert_fusion.1
  93.6 51.9 %all_to_all.20 = bf16[4,64,4096]{2,1,0:T(8,128)(2,1)S(1)} all-to-all(bf16[4,64,4096]{2,1,0:T(8,128)(2,1)S(1)} %convolution_convert_fusion.1), channel_id=1, replica_groups=mesh['groups'=2,'mp'=2,'expert'=4,'dp'=2] {'expert'}, dimensions={0} | all-to-all | bytes 4194304 | tf_op jit(solution)/shard_map/all_to_all | solution.py:49
  145.5 0.0 all-gather.15.cloned.1.call-done
  145.5 21.9 %fusion.10 = f32[256,3584]{1,0:T(8,128)} fusion(bf16[256,4096]{1,0:T(8,128)(2,1)S(1)} %bitcast.84, bf16[1,1,3584,4096]{3,2,1,0:T(8,128)(2,1)} %all-gather.15.cloned.1.call-done), kind=kOutput, calls=%fused_computation.10 | convolution fusion | flops 7516192768 | bytes 35127296 | tf_op jit(solution)/shard_map/dot_general | solution.py:54
  167.4 0.0 all-gather.17.cloned.1.call-done
  167.4 9.4 %all-gather.19.cloned.1.call-done = bf16[1,1,3584,4096]{3,2,1,0:T(8,128)(2,1)} async-done(((bf16[1,1,1792,4096]{3,2,1,0:T(8,128)(2,1)}), bf16[1,1,3584,4096]{3,2,1,0:T(8,128)(2,1)}) %all-gather.19.cloned.1.call-update) | async-done | bytes 29360144 | tf_op jit(solution)/shard_map/all_gather | solution.py:53
  176.8 29.7 %fusion.24 = bf16[256,4096]{1,0:T(8,128)(2,1)} fusion(bf16[1,1,3584,4096]{3,2,1,0:T(8,128)(2,1)} %all-gather.19.cloned.1.call-done, bf16[256,4096]{1,0:T(8,128)(2,1)S(1)} %bitcast.85, bf16[1,1,3584,4096]{3,2,1,0:T(8,128)(2,1)} %all-gather.17.cloned.1.call-done, f32[256,3584]{1,0:T(8,128)} %fusion.10), kind=kOutput, calls=%fused_computation.18 | convolution fusion | flops 15038939136 | bytes 66584576 | tf_op jit(solution)/shard_map/dot_general | solution.py:57
  206.5 0.0 reduce-scatter.3.cloned.1.call-update
  206.5 0.0 all-gather.21.cloned.1.call-start
  206.6 0.5 all-gather.21.cloned.1.call-update
  207.1 0.0 all-gather.23.cloned.1.call-start
  207.2 0.5 all-gather.23.cloned.1.call-update
  207.7 0.0 all-gather.25.cloned.1.call-start
  207.8 0.0 copy-start.2
  207.8 0.7 all-gather.25.cloned.1.call-update
  208.5 31.3 %reduce-scatter.3.cloned.1.call-done = bf16[256,2048]{1,0:T(8,128)(2,1)} async-done(((bf16[256,4096]{1,0:T(8,128)(2,1)}), bf16[256,2048]{1,0:T(8,128)(2,1)}) %reduce-scatter.3.cloned.1.call-update) | async-done | bytes 1048592 | tf_op jit(solution)/shard_map/reduce_scatter | solution.py:58
  239.8 4.6 all-to-all-start.1
  244.4 0.1 copy.23
  244.5 0.1 reduce_window_sum.18
  244.6 0.1 copy.25
  244.7 4.4 all-gather.4
  249.0 0.0 copy-done.2
  249.1 20.8 %all-to-all-done.1 = bf16[4,64,2048]{2,1,0:T(8,128)(2,1)S(1)} async-done(((bf16[4,64,2048]{2,1,0:T(8,128)(2,1)}), bf16[4,64,2048]{2,1,0:T(8,128)(2,1)S(1)}, u32[]{:S(2)}, u32[]{:S(2)}) %all-to-all-start.1) | async-done | bytes 1048608 | tf_op jit(solution)/shard_map/all_to_all | solution.py:61
  269.9 0.8 fusion.33
  270.7 8.0 %all_gather.35 = bf16[64,4096]{1,0:T(8,128)(2,1)S(1)} all-gather(bf16[64,2048]{1,0:T(8,128)(2,1)S(1)} %fusion.33), channel_id=1, replica_groups=mesh['groups'=2,'mp'=2,'expert'=4,'dp'=2] {'mp'}, dimensions={1}, use_global_device_ids=true | all-gather | bytes 786432 | tf_op jit(solution)/shard_map/all_gather | solution.py:37
  278.7 0.2 fusion.41
  278.9 2.1 convolution_convert_fusion
  281.1 3.6 all-to-all-start.2
  284.7 0.2 reduce-scatter.5.cloned.1.call-start
  284.9 2.9 all-gather.21.cloned.1.call-done
  287.8 43.7 %all-to-all-done.2 = bf16[4,64,4096]{2,1,0:T(8,128)(2,1)S(1)} async-done(((bf16[4,64,4096]{2,1,0:T(8,128)(2,1)}), bf16[4,64,4096]{2,1,0:T(8,128)(2,1)S(1)}, u32[]{:S(2)}, u32[]{:S(2)}) %all-to-all-start.2) | async-done | bytes 2097184 | tf_op jit(solution)/shard_map/all_to_all | solution.py:49
  331.6 15.8 %fusion.4 = f32[256,3584]{1,0:T(8,128)} fusion(bf16[256,4096]{1,0:T(8,128)(2,1)S(1)} %bitcast.82, bf16[1,1,3584,4096]{3,2,1,0:T(8,128)(2,1)} %all-gather.21.cloned.1.call-done), kind=kOutput, calls=%fused_computation.4 | convolution fusion | flops 7516192768 | bytes 35127296 | tf_op jit(solution)/shard_map/dot_general | solution.py:54
  347.3 0.0 all-gather.23.cloned.1.call-done
  347.3 39.1 %all-gather.25.cloned.1.call-done = bf16[1,1,3584,4096]{3,2,1,0:T(8,128)(2,1)} async-done(((bf16[1,1,1792,4096]{3,2,1,0:T(8,128)(2,1)}), bf16[1,1,3584,4096]{3,2,1,0:T(8,128)(2,1)}) %all-gather.25.cloned.1.call-update) | async-done | bytes 29360144 | tf_op jit(solution)/shard_map/all_gather | solution.py:53
  386.5 29.7 %fusion.27 = bf16[256,4096]{1,0:T(8,128)(2,1)} fusion(bf16[1,1,3584,4096]{3,2,1,0:T(8,128)(2,1)} %all-gather.25.cloned.1.call-done, bf16[256,4096]{1,0:T(8,128)(2,1)S(1)} %bitcast.83, bf16[1,1,3584,4096]{3,2,1,0:T(8,128)(2,1)} %all-gather.23.cloned.1.call-done, f32[256,3584]{1,0:T(8,128)} %fusion.4), kind=kOutput, calls=%fused_computation.19 | convolution fusion | flops 15038939136 | bytes 66584576 | tf_op jit(solution)/shard_map/dot_general | solution.py:57
  416.2 0.0 reduce-scatter.5.cloned.1.call-update
  416.2 33.2 %reduce-scatter.5.cloned.1.call-done = bf16[256,2048]{1,0:T(8,128)(2,1)} async-done(((bf16[256,4096]{1,0:T(8,128)(2,1)}), bf16[256,2048]{1,0:T(8,128)(2,1)}) %reduce-scatter.5.cloned.1.call-update) | async-done | bytes 1048592 | tf_op jit(solution)/shard_map/reduce_scatter | solution.py:58
  449.4 4.6 all-to-all-start.3
  454.0 25.6 %all-to-all-done.3 = bf16[4,64,2048]{2,1,0:T(8,128)(2,1)S(1)} async-done(((bf16[4,64,2048]{2,1,0:T(8,128)(2,1)}), bf16[4,64,2048]{2,1,0:T(8,128)(2,1)S(1)}, u32[]{:S(2)}, u32[]{:S(2)}) %all-to-all-start.3) | async-done | bytes 1048608 | tf_op jit(solution)/shard_map/all_to_all | solution.py:61
  479.6 1.5 fusion.32
  (17 shorter events, 0.2 us)
Async XLA Ops:
  6.5 139.0 %all-gather.15.cloned.1.call-start = ((), (), s32[]{:S(2)}) async-start(), calls=%async_computation.8 | async-start | bytes 44040192 | tf_op jit(solution)/shard_map/all_gather | solution.py:51
  28.5 138.9 %all-gather.17.cloned.1.call-start = ((), (), s32[]{:S(2)}) async-start(), calls=%async_computation.9 | async-start | bytes 44040192 | tf_op jit(solution)/shard_map/all_gather | solution.py:52
  54.1 122.7 %all-gather.19.cloned.1.call-start = ((), (), s32[]{:S(2)}) async-start(), calls=%async_computation.10 | async-start | bytes 44040192 | tf_op jit(solution)/shard_map/all_gather | solution.py:53
  76.6 0.7 copy-start.4
  76.6 0.7 copy-start.3
  76.6 1.0 copy-start.1
  76.6 8.9 %copy-start = (bf16[64,2048]{1,0:T(8,128)(2,1)S(1)}, bf16[64,2048]{1,0:T(8,128)(2,1)}, u32[]{:S(2)}) copy-start(bf16[64,2048]{1,0:T(8,128)(2,1)} %param.8) | copy-start | bytes 786436
  76.6 163.2 %reduce-scatter.3.cloned.1.call-start = ((), (), s32[]{:S(2)}) async-start(), calls=%async_computation.6 | async-start | bytes 3145728 | tf_op jit(solution)/shard_map/reduce_scatter | solution.py:58
  206.5 81.3 %all-gather.21.cloned.1.call-start = ((), (), s32[]{:S(2)}) async-start(), calls=%async_computation.11 | async-start | bytes 44040192 | tf_op jit(solution)/shard_map/all_gather | solution.py:51
  207.1 140.2 %all-gather.23.cloned.1.call-start = ((), (), s32[]{:S(2)}) async-start(), calls=%async_computation.12 | async-start | bytes 44040192 | tf_op jit(solution)/shard_map/all_gather | solution.py:52
  207.7 178.8 %all-gather.25.cloned.1.call-start = ((), (), s32[]{:S(2)}) async-start(), calls=%async_computation.13 | async-start | bytes 44040192 | tf_op jit(solution)/shard_map/all_gather | solution.py:53
  207.8 41.3 %copy-start.2 = (s32[2,64,2]{1,2,0:T(2,128)S(1)}, s32[2,64,2]{1,2,0:T(2,128)}, u32[]{:S(2)}) copy-start(s32[2,64,2]{1,2,0:T(2,128)} %param.11) | copy-start | bytes 3076
  239.8 30.2 %all-to-all-start.1 = ((bf16[4,64,2048]{2,1,0:T(8,128)(2,1)}), bf16[4,64,2048]{2,1,0:T(8,128)(2,1)S(1)}, u32[]{:S(2)}, u32[]{:S(2)}) async-start(bf16[4,64,2048]{2,1,0:T(8,128)(2,1)} %bitcast.86), calls=%async_computation.2 | async-start | bytes 2097152 | tf_op jit(solution)/shard_map/all_to_all | solution.py:61
  281.1 50.5 %all-to-all-start.2 = ((bf16[4,64,4096]{2,1,0:T(8,128)(2,1)}), bf16[4,64,4096]{2,1,0:T(8,128)(2,1)S(1)}, u32[]{:S(2)}, u32[]{:S(2)}) async-start(bf16[4,64,4096]{2,1,0:T(8,128)(2,1)} %convolution_convert_fusion), calls=%async_computation.3 | async-start | bytes 4194304 | tf_op jit(solution)/shard_map/all_to_all | solution.py:49
  284.7 164.7 %reduce-scatter.5.cloned.1.call-start = ((), (), s32[]{:S(2)}) async-start(), calls=%async_computation.7 | async-start | bytes 3145728 | tf_op jit(solution)/shard_map/reduce_scatter | solution.py:58
  449.4 30.2 %all-to-all-start.3 = ((bf16[4,64,2048]{2,1,0:T(8,128)(2,1)}), bf16[4,64,2048]{2,1,0:T(8,128)(2,1)S(1)}, u32[]{:S(2)}, u32[]{:S(2)}) async-start(bf16[4,64,2048]{2,1,0:T(8,128)(2,1)} %bitcast.87), calls=%async_computation.5 | async-start | bytes 2097152 | tf_op jit(solution)/shard_map/all_to_all | solution.py:61
Sparse Core Ops, SparseCore 0:
  28.7 49.3 all-gather.14
  79.6 47.7 all-gather.16
  129.0 47.7 all-gather.18
  206.7 33.0 reduce-scatter.2
  241.2 46.6 all-gather.20
  289.3 47.7 all-gather.22
  338.6 47.7 all-gather.24
  416.3 33.0 reduce-scatter.4
where the time goes:
time: 488 us
  waiting for transfers between devices  208 us (43%)
  matrix products  102 us (21%)
  blocking collectives  79.1 us (16%)
  local copies, waits for them, and re-layouts  70.9 us (15%)
  between operations  13.6 us (3%)
  starting transfers between devices  13.2 us (3%)
    reduce_scatter x2, waiting for transfers between devices, body(): lax.psum_scatter(partial_value.astype(jnp.bfloat16), 'mp', scatter_dimens...  64.6 us
    dot_general x2, matrix products, body(): jnp.dot(hidden, down_rows, preferred_element_type=jnp.float32)  59.4 us
    all_to_all x1, blocking collectives, body(): lax.all_to_all(outgoing, 'expert', split_axis=0, concat_axis=0, tiled=True)  51.9 us
    all_gather x2, waiting for transfers between devices, body(): down_rows = lax.all_gather(w_down[layer_idx, 0], 'dp', axis=0, tiled=True)  48.5 us
    all_to_all x2, waiting for transfers between devices, body(): lax.all_to_all(summed.reshape(experts, tok_rows, slice_width), 'expert',...  46.4 us
    all_to_all x1, waiting for transfers between devices, body(): lax.all_to_all(outgoing, 'expert', split_axis=0, concat_axis=0, tiled=True)  43.7 us
    dot_general x2, matrix products, body(): lax.dot_general(inputs, gate_rows, contract, preferred_element_type=jnp.f...  37.7 us
    slice x1, local copies, waits for them, and re-layouts, body(): up_rows = lax.all_gather(w_up[layer_idx, 0], 'dp', axis=0, tiled=True)  25.5 us
  transfers between devices with their start and end apart: 11, of which 8 were waited for; matrix products, arithmetic and copies ran while one was open for 19% of the time, Pallas kernels for 0%

commit v1 on v0

v1 whole, which is shorter than its diff:
```python
import jax
import jax.numpy as jnp
from jax import lax
from jax.sharding import PartitionSpec as P

LAYERS = 2


norm_floor = 0.1


def body(hidden_in, norm_gain, expert_ids, gate_counts, exit_layer, w_gate, w_up, w_down):
    experts = lax.axis_size("expert")
    shards = lax.axis_size("mp")
    full_width = hidden_in.shape[1] * shards
    contract = (((1,), (1,)), ((), ()))
    expert_range = jnp.arange(experts, dtype=jnp.int32)
    counts = gate_counts.astype(jnp.float32)
    gate_share = counts / jnp.sum(counts, axis=2, keepdims=True)
    active = exit_layer[None, :] > jnp.arange(LAYERS, dtype=jnp.int32)[:, None]
    matched = (expert_ids[..., None] == expert_range) & active[:, :, None, None]
    weight = jnp.sum(jnp.where(matched, gate_share[..., None], jnp.float32(0.0)), axis=2)
    weight = lax.all_gather(weight, ("expert", "dp"), axis=1, tiled=True)
    weight = lax.dynamic_index_in_dim(weight, lax.axis_index("expert"), 2, keepdims=True)
    gain = lax.all_gather(norm_gain, "mp", axis=1, tiled=True).astype(jnp.float32)
    current = hidden_in
    for layer_idx in range(LAYERS):
        rows = lax.all_gather(current, "mp", axis=1, tiled=True)
        rows_f32 = rows.astype(jnp.float32)
        inv_rms = lax.rsqrt(jnp.sum(rows_f32 * rows_f32, axis=1) / full_width + norm_floor)
        normed = (rows_f32 * inv_rms[:, None] * gain[layer_idx][None, :]).astype(jnp.bfloat16)
        inputs = lax.all_gather(normed, ("expert", "dp"), axis=0, tiled=True)
        gate_val = lax.dot_general(
            inputs, w_gate[layer_idx, 0], contract, preferred_element_type=jnp.float32
        )
        up_val = lax.dot_general(
            inputs, w_up[layer_idx, 0], contract, preferred_element_type=jnp.float32
        )
        hidden = (jax.nn.silu(gate_val) * up_val * weight[layer_idx]).astype(jnp.bfloat16)
        partial_value = jnp.dot(
            hidden, w_down[layer_idx, 0], preferred_element_type=jnp.float32
        ).astype(jnp.bfloat16)
        summed = lax.psum_scatter(
            partial_value, ("expert", "dp"), scatter_dimension=0, tiled=True
        )
        summed = lax.psum_scatter(summed, "mp", scatter_dimension=1, tiled=True)
        current = (current.astype(jnp.float32) + summed.astype(jnp.float32)).astype(jnp.bfloat16)
    return current


def solution(mesh):
    in_specs = (
        P(("groups", "expert", "dp"), "mp"),
        P(None, "mp"),
        P(None, ("groups", "expert", "dp"), None),
        P(None, ("groups", "expert", "dp"), None),
        P(("groups", "expert", "dp")),
        P(None, "expert", ("mp", "dp"), None),
        P(None, "expert", ("mp", "dp"), None),
        P(None, "expert", ("mp", "dp"), None),
    )
    out_specs = P(("groups", "expert", "dp"), "mp")
    return jax.shard_map(body, mesh=mesh, in_specs=in_specs, out_specs=out_specs, check_vma=False)
```

time: 488 us -> 373 us (0.76)
  local copies, waits for them, and re-layouts: 70.9 us -> 4.08 us
  blocking collectives: 79.1 us -> 39.7 us
  starting transfers between devices: 13.2 us -> 0.21 us
  other arithmetic: 0.78 us -> 7.29 us
  waiting for transfers between devices: 208 us -> 203 us
    all_to_all x3 -> x0, waiting for transfers between devices: 90.1 us -> none  [the longest x2 46.4 us: body(): lax.all_to_all(summed.reshape(experts, tok_rows, slice_width), 'expert',...]
    slice x4 -> x2, local copies, waits for them, and re-layouts: 69.9 us -> 3.95 us  [the longest x1 3.93 us: body(): weight[layer_idx]]
    reduce_scatter x2 -> x4, waiting for transfers between devices: 64.6 us -> 129 us  [the longest x2 98.4 us: body(): lax.psum_scatter(partial_value, ('expert', 'dp'), scatter_dimension=0, ti...]
    all_to_all x1 -> x0, blocking collectives: 51.9 us -> none  [body(): lax.all_to_all(outgoing, 'expert', split_axis=0, concat_axis=0, tiled=True)]
    all_gather x6 -> x2, waiting for transfers between devices: 51.4 us -> 73.6 us  [body(): inputs = lax.all_gather(normed, ('expert', 'dp'), axis=0, tiled=True)]
    all_to_all x3 -> x0, starting transfers between devices: 12.8 us -> none  [the longest x2 9.17 us: body(): lax.all_to_all(summed.reshape(experts, tok_rows, slice_width), 'expert',...]
    all_gather x4, blocking collectives: 27.2 us -> 39.7 us  [the longest x1 17.3 us: body(): weight = lax.all_gather(weight, ('expert', 'dp'), axis=1, tiled=True)]
    dot_general x8 -> x4, matrix products: 102 us -> 106 us  [the longest x2 76.2 us: body(): jnp.dot(hidden, w_down[layer_idx, 0], preferred_element_type=jnp.float32)]
  transfers between devices with their start and end apart: 11 -> 6, of which waited for: 8 -> 6; matrix products, arithmetic and copies ran while one was open for 19% -> 2% of each run, Pallas kernels for 0% -> 0%
where the time goes in v1:
time: 373 us
  waiting for transfers between devices  203 us (54%)
  matrix products  106 us (28%)
  blocking collectives  39.7 us (11%)
  between operations  13.5 us (4%)
  other arithmetic  7.29 us (2%)
  local copies, waits for them, and re-layouts  4.08 us (1%)
    reduce_scatter x2, waiting for transfers between devices, body(): lax.psum_scatter(partial_value, ('expert', 'dp'), scatter_dimension=0, ti...  98.4 us
    dot_general x2, matrix products, body(): jnp.dot(hidden, w_down[layer_idx, 0], preferred_element_type=jnp.float32)  76.2 us
    all_gather x2, waiting for transfers between devices, body(): inputs = lax.all_gather(normed, ('expert', 'dp'), axis=0, tiled=True)  73.6 us
    reduce_scatter x2, waiting for transfers between devices, body(): summed = lax.psum_scatter(summed, 'mp', scatter_dimension=1, tiled=True)  30.5 us
    dot_general x2, matrix products, body(): lax.dot_general(inputs, w_gate[layer_idx, 0], contract, preferred_element...  29.3 us
    all_gather x1, blocking collectives, body(): weight = lax.all_gather(weight, ('expert', 'dp'), axis=1, tiled=True)  17.3 us
    all_gather x2, blocking collectives, body(): rows = lax.all_gather(current, 'mp', axis=1, tiled=True)  16.8 us
  transfers between devices with their start and end apart: 6, of which 6 were waited for; matrix products, arithmetic and copies ran while one was open for 2% of the time, Pallas kernels for 0%

profile of v1, /device:TPU:0, one launch (start us, length us, event | category | flops | bytes accessed | tf_op | source)
XLA Modules:
  0.0 372.9 jit_solution(15765500869376924986)
XLA Ops:
  6.5 0.0 all-gather.3.cloned.1.call-start
  6.5 5.6 %all_gather.19 = bf16[2,4096]{1,0:T(2,128)(2,1)S(1)} all-gather(bf16[2,2048]{1,0:T(2,128)(2,1)} %param.9), channel_id=1, replica_groups=mesh['groups'=2,'mp'=2,'expert'=4,'dp'=2] {'mp'}, dimensions={1}, use_global_device_ids=true | all-gather | bytes 24576 | tf_op jit(solution)/shard_map/all_gather | solution.py:25
  12.1 8.1 %all_gather.18 = bf16[64,4096]{1,0:T(8,128)(2,1)S(1)} all-gather(bf16[64,2048]{1,0:T(8,128)(2,1)} %param.8), channel_id=1, replica_groups=mesh['groups'=2,'mp'=2,'expert'=4,'dp'=2] {'mp'}, dimensions={1}, use_global_device_ids=true | all-gather | bytes 786432 | tf_op jit(solution)/shard_map/all_gather | solution.py:28
  20.2 0.2 fusion.34
  20.4 1.0 fusion.36
  21.4 0.0 all-gather.3.cloned.1.call-update
  21.4 0.0 reduce-scatter.5.cloned.1.call-start
  21.5 0.7 iota_compare_fusion.1
  22.1 0.8 convert_divide_fusion
  22.9 0.7 select_reduce_fusion
  23.6 0.1 copy.15
  23.7 17.3 %all_gather.21 = f32[2,512,4]{2,0,1:T(2,128)S(1)} all-gather(f32[2,64,4]{2,0,1:T(2,128)S(1)} %copy.15), channel_id=1, replica_groups=mesh['groups'=2,'mp'=2,'expert'=4,'dp'=2] {'expert','dp'}, dimensions={1}, use_global_device_ids=true | all-gather | bytes 18432 | tf_op jit(solution)/shard_map/all_gather | solution.py:23
  41.1 3.9 %dynamic-slice_reduce_fusion = (f32[512]{0:T(512)S(1)}, f32[512]{0:T(512)S(1)}) fusion(f32[2,512,4]{2,0,1:T(2,128)S(1)} %all_gather.21, s32[]{:T(128)S(6)} %add.48, s32[]{:T(128)S(6)} %select_n.9), kind=kLoop, calls=%fused_computation.36 | loop fusion | bytes 8200 | tf_op jit(solution)/shard_map/slice | solution.py:39
  45.0 26.7 %all-gather.3.cloned.1.call-done = bf16[512,4096]{1,0:T(8,128)(2,1)} async-done(((bf16[64,4096]{1,0:T(8,128)(2,1)}), bf16[512,4096]{1,0:T(8,128)(2,1)}) %all-gather.3.cloned.1.call-update) | async-done | bytes 4194320 | tf_op jit(solution)/shard_map/all_gather | solution.py:32
  71.6 14.6 %fusion.10 = f32[512,1792]{1,0:T(8,128)} fusion(bf16[512,4096]{1,0:T(8,128)(2,1)} %all-gather.3.cloned.1.call-done, bf16[2,1,1792,4096]{3,2,1,0:T(8,128)(2,1)} %param.13), kind=kOutput, calls=%fused_computation.10 | convolution fusion | flops 7516192768 | bytes 22544384 | tf_op jit(solution)/shard_map/dot_general | solution.py:33
  86.3 38.1 %fusion.18 = bf16[512,4096]{1,0:T(8,128)(2,1)} fusion(bf16[2,1,1792,4096]{3,2,1,0:T(8,128)(2,1)} %param.15, f32[512,1792]{1,0:T(8,128)} %fusion.10, bf16[512,4096]{1,0:T(8,128)(2,1)} %all-gather.3.cloned.1.call-done, bf16[2,1,1792,4096]{3,2,1,0:T(8,128)(2,1)} %param.14, f32[512]{0:T(512)S(1)} %get-tuple-element.6), kind=kOutput, calls=%fused_computation.18 | convolution fusion | flops 15040905216 | bytes 41420800 | tf_op jit(solution)/shard_map/dot_general | solution.py:40
  124.4 0.0 copy-start
  124.4 0.0 reduce-scatter.5.cloned.1.call-update
  124.4 0.0 reduce-scatter.7.cloned.1.call-start
  124.5 49.6 %reduce-scatter.5.cloned.1.call-done = bf16[64,4096]{1,0:T(8,128)(2,1)} async-done(((bf16[512,4096]{1,0:T(8,128)(2,1)}), bf16[64,4096]{1,0:T(8,128)(2,1)}) %reduce-scatter.5.cloned.1.call-update) | async-done | bytes 524304 | tf_op jit(solution)/shard_map/reduce_scatter | solution.py:43
  174.0 0.0 reduce-scatter.7.cloned.1.call-update
  174.0 0.0 all-gather.5.cloned.1.call-start
  174.1 15.3 %reduce-scatter.7.cloned.1.call-done = bf16[64,2048]{1,0:T(8,128)(2,1)} async-done(((bf16[64,4096]{1,0:T(8,128)(2,1)}), bf16[64,2048]{1,0:T(8,128)(2,1)}) %reduce-scatter.7.cloned.1.call-update) | async-done | bytes 262160 | tf_op jit(solution)/shard_map/reduce_scatter | solution.py:46
  189.4 0.0 copy-done
  189.4 1.0 add_convert_fusion.1
  190.4 8.7 %all_gather.22 = bf16[64,4096]{1,0:T(8,128)(2,1)S(1)} all-gather(bf16[64,2048]{1,0:T(8,128)(2,1)S(1)} %add_convert_fusion.1), channel_id=1, replica_groups=mesh['groups'=2,'mp'=2,'expert'=4,'dp'=2] {'mp'}, dimensions={1}, use_global_device_ids=true | all-gather | bytes 786432 | tf_op jit(solution)/shard_map/all_gather | solution.py:28
  199.2 0.2 fusion.37
  199.4 1.0 fusion.39
  200.4 0.0 all-gather.5.cloned.1.call-update
  200.4 0.0 reduce-scatter.9.cloned.1.call-start
  200.5 47.0 %all-gather.5.cloned.1.call-done = bf16[512,4096]{1,0:T(8,128)(2,1)} async-done(((bf16[64,4096]{1,0:T(8,128)(2,1)}), bf16[512,4096]{1,0:T(8,128)(2,1)}) %all-gather.5.cloned.1.call-update) | async-done | bytes 4194320 | tf_op jit(solution)/shard_map/all_gather | solution.py:32
  247.4 14.7 %fusion.4 = f32[512,1792]{1,0:T(8,128)} fusion(bf16[512,4096]{1,0:T(8,128)(2,1)} %all-gather.5.cloned.1.call-done, bf16[2,1,1792,4096]{3,2,1,0:T(8,128)(2,1)} %param.13), kind=kOutput, calls=%fused_computation.4 | convolution fusion | flops 7516192768 | bytes 22544384 | tf_op jit(solution)/shard_map/dot_general | solution.py:33
  262.1 38.1 %fusion.21 = bf16[512,4096]{1,0:T(8,128)(2,1)} fusion(bf16[2,1,1792,4096]{3,2,1,0:T(8,128)(2,1)} %param.15, f32[512,1792]{1,0:T(8,128)} %fusion.4, bf16[512,4096]{1,0:T(8,128)(2,1)} %all-gather.5.cloned.1.call-done, bf16[2,1,1792,4096]{3,2,1,0:T(8,128)(2,1)} %param.14, f32[512]{0:T(512)S(1)} %get-tuple-element.5), kind=kOutput, calls=%fused_computation.19 | convolution fusion | flops 15040905216 | bytes 41420800 | tf_op jit(solution)/shard_map/dot_general | solution.py:40
  300.2 0.0 reduce-scatter.9.cloned.1.call-update
  300.2 0.0 reduce-scatter.11.cloned.1.call-start
  300.2 48.8 %reduce-scatter.9.cloned.1.call-done = bf16[64,4096]{1,0:T(8,128)(2,1)} async-done(((bf16[512,4096]{1,0:T(8,128)(2,1)}), bf16[64,4096]{1,0:T(8,128)(2,1)}) %reduce-scatter.9.cloned.1.call-update) | async-done | bytes 524304 | tf_op jit(solution)/shard_map/reduce_scatter | solution.py:43
  349.1 0.0 reduce-scatter.11.cloned.1.call-update
  349.1 15.2 %reduce-scatter.11.cloned.1.call-done = bf16[64,2048]{1,0:T(8,128)(2,1)} async-done(((bf16[64,4096]{1,0:T(8,128)(2,1)}), bf16[64,2048]{1,0:T(8,128)(2,1)}) %reduce-scatter.11.cloned.1.call-update) | async-done | bytes 262160 | tf_op jit(solution)/shard_map/reduce_scatter | solution.py:46
  364.3 1.7 add_convert_fusion
  (3 shorter events, 0.0 us)
Async XLA Ops:
  6.5 65.1 %all-gather.3.cloned.1.call-start = ((), (), s32[]{:S(2)}) async-start(), calls=%async_computation.4 | async-start | bytes 4718592 | tf_op jit(solution)/shard_map/all_gather | solution.py:32
  21.4 152.6 %reduce-scatter.5.cloned.1.call-start = ((), (), s32[]{:S(2)}) async-start(), calls=%async_computation.5 | async-start | bytes 4718592 | tf_op jit(solution)/shard_map/reduce_scatter | solution.py:43
  124.4 65.0 %copy-start = (bf16[64,2048]{1,0:T(8,128)(2,1)S(1)}, bf16[64,2048]{1,0:T(8,128)(2,1)}, u32[]{:S(2)}) copy-start(bf16[64,2048]{1,0:T(8,128)(2,1)} %param.8) | copy-start | bytes 786436
  124.4 65.0 %reduce-scatter.7.cloned.1.call-start = ((), (), s32[]{:S(2)}) async-start(), calls=%async_computation.6 | async-start | bytes 786432 | tf_op jit(solution)/shard_map/reduce_scatter | solution.py:46
  174.0 73.4 %all-gather.5.cloned.1.call-start = ((), (), s32[]{:S(2)}) async-start(), calls=%async_computation.7 | async-start | bytes 4718592 | tf_op jit(solution)/shard_map/all_gather | solution.py:32
  200.4 148.7 %reduce-scatter.9.cloned.1.call-start = ((), (), s32[]{:S(2)}) async-start(), calls=%async_computation.8 | async-start | bytes 4718592 | tf_op jit(solution)/shard_map/reduce_scatter | solution.py:43
  300.2 64.1 %reduce-scatter.11.cloned.1.call-start = ((), (), s32[]{:S(2)}) async-start(), calls=%async_computation.9 | async-start | bytes 786432 | tf_op jit(solution)/shard_map/reduce_scatter | solution.py:46
Sparse Core Ops, SparseCore 0:
  21.5 50.0 all-gather.2
  124.5 49.4 reduce-scatter.4
  176.3 13.0 reduce-scatter.6
  200.5 46.8 all-gather.4
  300.3 48.7 reduce-scatter.8
  351.2 13.0 reduce-scatter.10

commit v2 on v1

v2 whole, which is shorter than its diff:
```python
import functools

import jax
import jax.numpy as jnp
from jax import lax
from jax.experimental import pallas as pl
from jax.experimental.pallas import tpu as pltpu
from jax.sharding import PartitionSpec as P

LAYERS = 2


norm_floor = 0.1
MESH = pl.DeviceIdType.MESH
CHUNK = 16


def tile_of(length, best):
    tile = best
    while tile >= 128:
        if length % tile == 0:
            return tile
        tile //= 2
    return length


def layer_kernel(
    layer_idx, n, dp, mp,
    cur_ref, gain_ref, share_ref, wg_hbm, wu_hbm, wd_hbm, out_ref,
    wg, wu, wd, x, p, rd, rcw, rcc, xr, normed, hid, col,
    local_sem, w_sem, x_s, x_r, zcw_s, zcw_r, zcc_s, zcc_r, dp_s, dp_r,
    rd_s, rd_r, rcw_s, rcw_r, rcc_s, rcc_r, xr_s, xr_r,
):
    rows, width = cur_ref.shape
    full = width * mp
    units = wg.shape[0]
    pair = dp * rows
    e, m, d = lax.axis_index("expert"), lax.axis_index("mp"), lax.axis_index("dp")
    half = n // 2
    first, second = list(range(mp // 2)), list(range(mp // 2, mp))
    every = list(range(mp))

    def block(offset):
        return lax.rem(e + offset + n, n)

    def part(r):
        return lax.rem(m - r + mp, mp)

    def core(k):
        return lax.rem(d + k, dp)

    up_z, down_z = {"expert": block(1)}, {"expert": block(-1)}

    def remote(src, dst, ss, rs, dev):
        return pltpu.make_async_remote_copy(
            src_ref=src, dst_ref=dst, send_sem=ss, recv_sem=rs, device_id=dev, device_id_type=MESH
        )

    sent = []

    def send(copy):
        copy.start()
        sent.append(copy)

    def travels(j, going_up):
        if 2 * j == n:
            return first if going_up else second
        return every

    weights = []
    for i, (src, dst) in enumerate(((wg_hbm, wg), (wu_hbm, wu), (wd_hbm, wd))):
        copy = pltpu.make_async_copy(src.at[layer_idx, 0], dst, w_sem.at[i])
        copy.start()
        weights.append(copy)
    mine = pltpu.make_async_copy(cur_ref, x.at[e, d, m], local_sem.at[0])
    mine.start()

    barrier = pltpu.get_barrier_semaphore()
    peers = [{"mp": part(r)} for r in range(1, mp)] + [up_z, down_z]
    peers += [{"dp": core(k)} for k in range(1, dp)]
    for dev in peers:
        pl.semaphore_signal(barrier, inc=1, device_id=dev, device_id_type=MESH)
    pl.semaphore_wait(barrier, len(peers))
    mine.wait()

    def cw(j, r, blk):
        ref = x.at[blk, d, part(r)]
        return remote(ref, ref, zcw_s.at[j, r], zcw_r.at[j, r], up_z)

    def cc(j, r, blk):
        ref = x.at[blk, d, part(r)]
        return remote(ref, ref, zcc_s.at[j, r], zcc_r.at[j, r], down_z)

    def to_core(level_slot, r, blk):
        for k in range(1, dp):
            ref = x.at[blk, d, part(r)]
            send(remote(ref, ref, dp_s.at[level_slot, r, k], dp_r.at[level_slot, r, k],
                        {"dp": core(k)}))

    def from_core(level_slot, blk):
        for r in every:
            for k in range(1, dp):
                ref = x.at[blk, core(dp - k), part(r)]
                remote(ref, ref, dp_s.at[level_slot, r, k], dp_r.at[level_slot, r, k],
                       {"dp": core(k)}).wait_recv()

    for r in every:
        if r == 0:
            for q in range(1, mp):
                ref = x.at[e, d, m]
                send(remote(ref, ref, x_s.at[q], x_r.at[q], {"mp": lax.rem(m + q, mp)}))
        else:
            ref = x.at[e, d, part(r)]
            remote(ref, ref, x_s.at[r], x_r.at[r], {"mp": lax.rem(m + r, mp)}).wait_recv()
        if r in travels(1, True):
            send(cw(1, r, e))
        if r in travels(1, False):
            send(cc(1, r, e))
        to_core(0, r, e)

    def norm(place, blk):
        for c in range(dp):
            base = place * pair + c * rows
            col[base:base + rows, :] = share_ref[blk, c]

            def chunk(i, _):
                at = pl.ds(pl.multiple_of(i * CHUNK, CHUNK), CHUNK)
                total = jnp.zeros((CHUNK, 1), jnp.float32)
                for q in every:
                    v = x[blk, c, q, at, :].astype(jnp.float32)
                    total = total + jnp.sum(v * v, axis=1, keepdims=True)
                inv = lax.rsqrt(total / full + norm_floor)
                to = pl.ds(pl.multiple_of(base + i * CHUNK, CHUNK), CHUNK)
                for q in every:
                    v = x[blk, c, q, at, :].astype(jnp.float32)
                    normed[to, q * width:(q + 1) * width] = (v * inv * gain_ref[q]).astype(
                        jnp.bfloat16
                    )
                return 0

            lax.fori_loop(0, rows // CHUNK, chunk, 0)

    tile = tile_of(units, 256)
    contract = (((1,), (1,)), ((), ()))

    def hidden(start, blocks):
        for place, blk in enumerate(blocks):
            norm(place, blk)
        size = pair * len(blocks)

        def step(t, _):
            at = pl.ds(pl.multiple_of(t * tile, tile), tile)
            a = normed[0:size, :]
            g = lax.dot_general(a, wg[at, :], contract, preferred_element_type=jnp.float32)
            u = lax.dot_general(a, wu[at, :], contract, preferred_element_type=jnp.float32)
            h = g / (1.0 + jnp.exp(-g)) * u * col[0:size, :]
            hid[start:start + size, at] = h.astype(jnp.bfloat16)
            return 0

        if tile == units:
            a = normed[0:size, :]
            g = lax.dot_general(a, wg[...], contract, preferred_element_type=jnp.float32)
            u = lax.dot_general(a, wu[...], contract, preferred_element_type=jnp.float32)
            h = g / (1.0 + jnp.exp(-g)) * u * col[0:size, :]
            hid[start:start + size, :] = h.astype(jnp.bfloat16)
        else:
            lax.fori_loop(0, units // tile, step, 0)

    def level_blocks(j):
        if j == 0:
            return [e]
        if 2 * j == n:
            return [block(j)]
        return [block(-j), block(j)]

    starts, slots, filled, slot = [], [], 0, 0
    for j in range(half + 1):
        starts.append(filled)
        slots.append(slot)
        count = 1 if j == 0 or 2 * j == n else 2
        filled += count * pair
        slot += count

    from_core(0, e)
    weights[0].wait()
    weights[1].wait()
    hidden(0, [e])
    for j in range(1, half + 1):
        blocks = level_blocks(j)
        low, high = slots[j], slots[j] + len(blocks) - 1
        for r in every:
            if r in travels(j, True):
                cw(j, r, block(-j)).wait_recv()
                if j < half and r in travels(j + 1, True):
                    send(cw(j + 1, r, block(-j)))
                to_core(low, r, block(-j))
            if r in travels(j, False):
                cc(j, r, block(j)).wait_recv()
                if j < half and r in travels(j + 1, False):
                    send(cc(j + 1, r, block(j)))
                to_core(high, r, block(j))
        for i, blk in enumerate(blocks):
            from_core(low + i, blk)
        hidden(starts[j], blocks)

    weights[2].wait()
    ctile = tile_of(width, 256)

    def project(start, blocks):
        size = pair * len(blocks)
        for q in every:
            def step(t, _):
                at = pl.ds(pl.multiple_of(t * ctile, ctile), ctile)
                wide = pl.ds(pl.multiple_of(q * width + t * ctile, ctile), ctile)
                y = jnp.dot(hid[start:start + size, :], wd[:, wide],
                            preferred_element_type=jnp.float32).astype(jnp.bfloat16)
                for i, blk in enumerate(blocks):
                    for c in range(dp):
                        base = i * pair + c * rows
                        p[blk, c, q, :, at] = y[base:base + rows]
                return 0

            lax.fori_loop(0, width // ctile, step, 0)

    def add(blk, q, others):
        def chunk(i, _):
            at = pl.ds(pl.multiple_of(i * CHUNK, CHUNK), CHUNK)
            v = p[blk, d, q, at, :].astype(jnp.float32)
            for ref, index in others:
                v = v + ref[index + (at, slice(None))].astype(jnp.float32)
            p[blk, d, q, at, :] = v.astype(jnp.bfloat16)
            return 0

        lax.fori_loop(0, rows // CHUNK, chunk, 0)

    def back_cw(j, r, blk):
        return remote(p.at[blk, d, part(r)], rcw.at[j - 1, r], rcw_s.at[j, r], rcw_r.at[j, r], up_z)

    def back_cc(j, r, blk):
        return remote(p.at[blk, d, part(r)], rcc.at[j - 1, r], rcc_s.at[j, r], rcc_r.at[j, r], down_z)

    def swap(slot, k, blk):
        return remote(p.at[blk, core(k)], rd.at[slot, k - 1], rd_s.at[slot, k], rd_r.at[slot, k],
                      {"dp": core(k)})

    late_first = every[1:] + every[:1]
    x_back = []
    for j in range(half, -1, -1):
        blocks = level_blocks(j)
        project(starts[j], blocks)
        for i, blk in enumerate(blocks):
            for k in range(1, dp):
                send(swap(slots[j] + i, k, blk))
        for i, blk in enumerate(blocks):
            for k in range(1, dp):
                swap(slots[j] + i, k, blk).wait_recv()
        for r in late_first:
            q = part(r)
            for i, blk in enumerate(blocks):
                others = [(rd, (slots[j] + i, k - 1, q)) for k in range(1, dp)]
                upward = j > 0 and (len(blocks) == 1 or i == 1)
                downward = j > 0 and (len(blocks) == 1 or i == 0)
                if j < half and (upward or j == 0) and r in travels(j + 1, True):
                    back_cw(j + 1, r, blk).wait_recv()
                    others.append((rcw, (j, r)))
                if j < half and (downward or j == 0) and r in travels(j + 1, False):
                    back_cc(j + 1, r, blk).wait_recv()
                    others.append((rcc, (j, r)))
                add(blk, q, others)
                if upward and r in travels(j, True):
                    send(back_cw(j, r, blk))
                if downward and r in travels(j, False):
                    send(back_cc(j, r, blk))
                if j == 0 and r > 0:
                    copy = remote(p.at[e, d, q], xr.at[r], xr_s.at[r], xr_r.at[r], {"mp": q})
                    send(copy)
                    x_back.append(copy)
    for copy in x_back:
        copy.wait_recv()

    def last(i, _):
        at = pl.ds(pl.multiple_of(i * CHUNK, CHUNK), CHUNK)
        v = p[e, d, m, at, :].astype(jnp.float32)
        for r in range(1, mp):
            v = v + xr[r, at, :].astype(jnp.float32)
        out_ref[at, :] = (cur_ref[at, :].astype(jnp.float32) + v).astype(jnp.bfloat16)
        return 0

    lax.fori_loop(0, rows // CHUNK, last, 0)
    for copy in sent:
        copy.wait_send()


def layer(layer_idx, n, dp, mp, current, gain, share, w_gate, w_up, w_down):
    rows, width = current.shape
    units, full = w_gate.shape[2:]
    half = n // 2
    bf, dma = jnp.bfloat16, pltpu.SemaphoreType.DMA
    vmem = pl.BlockSpec(memory_space=pltpu.VMEM)
    hbm = pl.BlockSpec(memory_space=pl.ANY)
    return pl.pallas_call(
        functools.partial(layer_kernel, layer_idx, n, dp, mp),
        out_shape=jax.ShapeDtypeStruct((rows, width), bf),
        in_specs=[vmem, vmem, vmem, hbm, hbm, hbm],
        out_specs=vmem,
        scratch_shapes=[
            pltpu.VMEM((units, full), bf),
            pltpu.VMEM((units, full), bf),
            pltpu.VMEM((units, full), bf),
            pltpu.VMEM((n, dp, mp, rows, width), bf),
            pltpu.VMEM((n, dp, mp, rows, width), bf),
            pltpu.VMEM((n, max(dp - 1, 1), mp, rows, width), bf),
            pltpu.VMEM((half, mp, rows, width), bf),
            pltpu.VMEM((half, mp, rows, width), bf),
            pltpu.VMEM((mp, rows, width), bf),
            pltpu.VMEM((2 * dp * rows, full), bf),
            pltpu.VMEM((n * dp * rows, units), bf),
            pltpu.VMEM((2 * dp * rows, 1), jnp.float32),
            dma((1,)), dma((3,)), dma((mp,)), dma((mp,)),
            dma((half + 1, mp)), dma((half + 1, mp)), dma((half + 1, mp)), dma((half + 1, mp)),
            dma((n, mp, dp)), dma((n, mp, dp)), dma((n, dp)), dma((n, dp)),
            dma((half + 1, mp)), dma((half + 1, mp)), dma((half + 1, mp)), dma((half + 1, mp)),
            dma((mp,)), dma((mp,)),
        ],
        compiler_params=pltpu.CompilerParams(
            collective_id=layer_idx, has_side_effects=True, vmem_limit_bytes=67043328
        ),
    )(current, gain, share, w_gate, w_up, w_down)


def body(hidden_in, norm_gain, expert_ids, gate_counts, exit_layer, w_gate, w_up, w_down):
    n, dp, mp = lax.axis_size("expert"), lax.axis_size("dp"), lax.axis_size("mp")
    rows, width = hidden_in.shape
    expert_range = jnp.arange(n, dtype=jnp.int32)
    counts = gate_counts.astype(jnp.float32)
    gate_share = counts / jnp.sum(counts, axis=2, keepdims=True)
    active = exit_layer[None, :] > jnp.arange(LAYERS, dtype=jnp.int32)[:, None]
    matched = (expert_ids[..., None] == expert_range) & active[:, :, None, None]
    share = jnp.sum(jnp.where(matched, gate_share[..., None], jnp.float32(0.0)), axis=2)
    share = lax.all_gather(share, ("expert", "dp"), axis=1, tiled=True)
    share = lax.dynamic_index_in_dim(share, lax.axis_index("expert"), 2, keepdims=True)
    share = share.reshape(LAYERS, n, dp, rows, 1)
    gain = lax.all_gather(norm_gain, "mp", axis=1, tiled=True).astype(jnp.float32)
    gain = gain.reshape(LAYERS, mp, 1, width)
    current = hidden_in
    for layer_idx in range(LAYERS):
        current = layer(
            layer_idx, n, dp, mp, current, gain[layer_idx], share[layer_idx], w_gate, w_up, w_down
        )
    return current


def solution(mesh):
    in_specs = (
        P(("groups", "expert", "dp"), "mp"),
        P(None, "mp"),
        P(None, ("groups", "expert", "dp"), None),
        P(None, ("groups", "expert", "dp"), None),
        P(("groups", "expert", "dp")),
        P(None, "expert", ("mp", "dp"), None),
        P(None, "expert", ("mp", "dp"), None),
        P(None, "expert", ("mp", "dp"), None),
    )
    out_specs = P(("groups", "expert", "dp"), "mp")
    return jax.shard_map(body, mesh=mesh, in_specs=in_specs, out_specs=out_specs, check_vma=False)
```

time: 373 us -> 227 us (0.61)
  waiting for transfers between devices: 203 us -> 0 us
  Pallas kernels: 0 us -> 199 us
  matrix products: 106 us -> 0 us
  blocking collectives: 39.7 us -> 21.1 us
  between operations: 13.5 us -> 0.03 us
  other arithmetic: 7.29 us -> 2.13 us
    pallas_call x0 -> x2, Pallas kernels: none -> 199 us  [layer(): pl.pallas_call(functools.partial(layer_kernel, layer_idx, n, dp, mp), out...]
    reduce_scatter x4 -> x0, waiting for transfers between devices: 129 us -> none  [the longest x2 98.4 us: body(): lax.psum_scatter(partial_value, ('expert', 'dp'), scatter_dimension=0, ti...]
    dot_general x4 -> x0, matrix products: 106 us -> none  [the longest x2 76.2 us: body(): jnp.dot(hidden, w_down[layer_idx, 0], preferred_element_type=jnp.float32)]
    all_gather x2 -> x0, waiting for transfers between devices: 73.6 us -> none  [body(): inputs = lax.all_gather(normed, ('expert', 'dp'), axis=0, tiled=True)]
    all_gather x3 -> x1, blocking collectives: 34.1 us -> 16.5 us  [body(): share = lax.all_gather(share, ('expert', 'dp'), axis=1, tiled=True)]
    convert_element_type x4 -> x0, other arithmetic: 4.72 us -> none  [the longest x2 2.73 us: body(): (current.astype(jnp.float32) + summed.astype(jnp.float32)).astype(jnp.bfl...]
  transfers between devices with their start and end apart: 6 -> 0, of which waited for: 6 -> 0; matrix products, arithmetic and copies ran while one was open for 2% -> 0% of each run, Pallas kernels for 0% -> 0%
where the time goes in v2:
time: 227 us
  Pallas kernels  199 us (88%)
  blocking collectives  21.1 us (9%)
  local copies, waits for them, and re-layouts  4.35 us (2%)
    pallas_call x2, Pallas kernels, layer(): pl.pallas_call(functools.partial(layer_kernel, layer_idx, n, dp, mp), out...  199 us
    all_gather x1, blocking collectives, body(): share = lax.all_gather(share, ('expert', 'dp'), axis=1, tiled=True)  16.5 us
    all_gather x1, blocking collectives, body(): lax.all_gather(norm_gain, 'mp', axis=1, tiled=True).astype(jnp.float32)  4.56 us

profile of v2, /device:TPU:0, one launch (start us, length us, event | category | flops | bytes accessed | tf_op | source)
XLA Modules:
  0.0 226.6 jit_solution(16062514819883000128)
XLA Ops:
  0.0 0.8 convert_divide_fusion
  0.8 0.7 iota_compare_fusion.1
  1.4 0.7 select_reduce_fusion
  2.1 0.1 copy.19
  2.3 16.5 %all_gather.7 = f32[2,512,4]{2,0,1:T(2,128)S(1)} all-gather(f32[2,64,4]{2,0,1:T(2,128)S(1)} %copy.19), channel_id=1, replica_groups=mesh['groups'=2,'mp'=2,'expert'=4,'dp'=2] {'expert','dp'}, dimensions={1}, use_global_device_ids=true | all-gather | bytes 18432 | tf_op jit(solution)/shard_map/all_gather | solution.py:340
  18.8 1.9 constant_dynamic-slice_fusion.1
  20.7 4.6 %all_gather.6 = bf16[2,4096]{1,0:T(2,128)(2,1)S(1)} all-gather(bf16[2,2048]{1,0:T(2,128)(2,1)} %param.9), channel_id=1, replica_groups=mesh['groups'=2,'mp'=2,'expert'=4,'dp'=2] {'mp'}, dimensions={1}, use_global_device_ids=true | all-gather | bytes 24576 | tf_op jit(solution)/shard_map/all_gather | solution.py:343
  25.3 0.6 fusion.6
  25.9 100.1 %shard_map.82.cur_ref = bf16[64,2048]{1,0:T(8,128)(2,1)} custom-call(bf16[64,2048]{1,0:T(8,128)(2,1)} %cur_ref.1, f32[2,1,2048]{2,1,0:T(1,128)} %bitcast.7, f32[4,2,64,1]{3,2,1,0:T(8,128)} %bitcast.5, bf16[2,1,1792,4096]{3,2,1,0:T(8,128)(2,1)} %wg_hbm.3, bf16[2,1,1792,4096]{3,2,1,0:T(8,128)(2,1)} %wu_hbm.3, bf16[2,1,1792,4096]{3,2,1,0:T(8,128)(2,1)} %wd_hbm.3), custom_call_target="tpu_custom_call" | custom-call | tf_op jit(solution)/shard_map/pallas_call | solution.py:301
  126.0 98.9 %shard_map.83 = bf16[64,2048]{1,0:T(8,128)(2,1)} custom-call(bf16[64,2048]{1,0:T(8,128)(2,1)} %shard_map.82.cur_ref, f32[2,1,2048]{2,1,0:T(1,128)} %bitcast.6, f32[4,2,64,1]{3,2,1,0:T(8,128)} %bitcast.4, bf16[2,1,1792,4096]{3,2,1,0:T(8,128)(2,1)} %wg_hbm.3, bf16[2,1,1792,4096]{3,2,1,0:T(8,128)(2,1)} %wu_hbm.3, bf16[2,1,1792,4096]{3,2,1,0:T(8,128)(2,1)} %wd_hbm.3), custom_call_target="tpu_custom_call" | custom-call | tf_op jit(solution)/shard_map/pallas_call | solution.py:301
  224.9 1.7 copy.23

commit v3 on v2

v3 whole, which is shorter than its diff:
```python
import functools

import jax
import jax.numpy as jnp
from jax import lax
from jax.experimental import pallas as pl
from jax.experimental.pallas import tpu as pltpu
from jax.sharding import PartitionSpec as P

LAYERS = 2


norm_floor = 0.1
MESH = pl.DeviceIdType.MESH
CHUNK = 16


def tile_of(length, best):
    tile = best
    while tile >= 128:
        if length % tile == 0:
            return tile
        tile //= 2
    return length


def layer_kernel(
    layer_idx, n, dp, mp,
    cur_ref, gain_ref, share_ref, wg_hbm, wu_hbm, wd_hbm, out_ref,
    wg, wu, wd, x, p, rd, rcw, rcc, xr, normed, hid, col, gains, shares,
    local_sem, w_sem, x_s, x_r, zcw_s, zcw_r, zcc_s, zcc_r, dp_s, dp_r,
    sd_s, sd_r, sz_s, sz_r, g_s, g_r, rd_s, rd_r, rcw_s, rcw_r, rcc_s, rcc_r, xr_s, xr_r,
):
    rows, width = cur_ref.shape
    full = width * mp
    units = wg.shape[0]
    pair = dp * rows
    e, m, d = lax.axis_index("expert"), lax.axis_index("mp"), lax.axis_index("dp")
    half = n // 2
    every = list(range(mp))

    def block(offset):
        return lax.rem(e + offset + n, n)

    def part(r):
        return lax.rem(m - r + mp, mp)

    def core(k):
        return lax.rem(d + k, dp)

    up_z, down_z = {"expert": block(1)}, {"expert": block(-1)}

    def remote(src, dst, ss, rs, dev):
        return pltpu.make_async_remote_copy(
            src_ref=src, dst_ref=dst, send_sem=ss, recv_sem=rs, device_id=dev, device_id_type=MESH
        )

    sent = []

    def send(copy):
        copy.start()
        sent.append(copy)

    weights = []
    for i, (src, dst) in enumerate(((wg_hbm, wg), (wu_hbm, wu), (wd_hbm, wd))):
        copy = pltpu.make_async_copy(src.at[layer_idx, 0], dst, w_sem.at[i])
        copy.start()
        weights.append(copy)
    mine = pltpu.make_async_copy(cur_ref, x.at[e, d, m], local_sem.at[0])
    mine.start()
    own_gain = pltpu.make_async_copy(gain_ref, gains.at[m], local_sem.at[1])
    own_gain.start()
    own_share = pltpu.make_async_copy(share_ref, shares.at[e, d], local_sem.at[2])
    own_share.start()

    barrier = pltpu.get_barrier_semaphore()
    peers = [{"mp": part(r)} for r in range(1, mp)] + [{"expert": block(k)} for k in range(1, n)]
    peers += [{"dp": core(k)} for k in range(1, dp)]
    for dev in peers:
        pl.semaphore_signal(barrier, inc=1, device_id=dev, device_id_type=MESH)
    pl.semaphore_wait(barrier, len(peers))
    mine.wait()
    own_gain.wait()
    own_share.wait()

    def piece(ref, j, going_up):
        if 2 * j == n:
            return ref.at[pl.ds(0 if going_up else rows // 2, rows // 2)]
        return ref

    def cw(j, blk):
        ref = piece(x.at[blk, d, m], j, True)
        return remote(ref, ref, zcw_s.at[j], zcw_r.at[j], up_z)

    def cc(j, blk):
        ref = piece(x.at[blk, d, m], j, False)
        return remote(ref, ref, zcc_s.at[j], zcc_r.at[j], down_z)

    def to_core(slot, r, blk):
        for k in range(1, dp):
            ref = x.at[blk, d, part(r)]
            send(remote(ref, ref, dp_s.at[slot, r, k], dp_r.at[slot, r, k], {"dp": core(k)}))

    def from_core(slot, blk):
        for k in range(1, dp):
            for r in every:
                ref = x.at[blk, core(dp - k), part(r)]
                remote(ref, ref, dp_s.at[slot, r, k], dp_r.at[slot, r, k],
                       {"dp": core(k)}).wait_recv()
            ref = shares.at[blk, core(dp - k)]
            remote(ref, ref, sd_s.at[slot, k], sd_r.at[slot, k], {"dp": core(k)}).wait_recv()

    def to_mp(slot, blk):
        for r in range(1, mp):
            ref = x.at[blk, d, m]
            send(remote(ref, ref, x_s.at[slot, r], x_r.at[slot, r], {"mp": lax.rem(m + r, mp)}))

    def from_mp(slot, blk):
        for r in range(1, mp):
            ref = x.at[blk, d, part(r)]
            remote(ref, ref, x_s.at[slot, r], x_r.at[slot, r],
                   {"mp": lax.rem(m + r, mp)}).wait_recv()
            to_core(slot, r, blk)

    def share_core(slot, blk):
        for k in range(1, dp):
            ref = shares.at[blk, d]
            send(remote(ref, ref, sd_s.at[slot, k], sd_r.at[slot, k], {"dp": core(k)}))

    def level_blocks(j):
        if j == 0:
            return [e]
        if 2 * j == n:
            return [block(j)]
        return [block(-j), block(j)]

    starts, slots, filled, slot = [], [], 0, 0
    for j in range(half + 1):
        starts.append(filled)
        slots.append(slot)
        count = 1 if j == 0 or 2 * j == n else 2
        filled += count * pair
        slot += count

    for r in range(1, mp):
        ref = gains.at[m]
        send(remote(ref, ref, g_s.at[r], g_r.at[r], {"mp": lax.rem(m + r, mp)}))
    for k in range(1, n):
        ref = shares.at[e, d]
        send(remote(ref, ref, sz_s.at[k], sz_r.at[k], {"expert": block(k)}))
    to_mp(0, e)
    send(cw(1, e))
    send(cc(1, e))
    share_core(0, e)
    to_core(0, 0, e)

    def arrive(j):
        blocks = level_blocks(j)
        low, high = slots[j], slots[j] + len(blocks) - 1
        cw(j, block(-j)).wait_recv()
        if j < half:
            send(cw(j + 1, block(-j)))
        if low != high:
            to_mp(low, block(-j))
            to_core(low, 0, block(-j))
        cc(j, block(j)).wait_recv()
        if j < half:
            send(cc(j + 1, block(j)))
        to_mp(high, block(j))
        to_core(high, 0, block(j))

    for r in range(1, mp):
        ref = gains.at[part(r)]
        remote(ref, ref, g_s.at[r], g_r.at[r], {"mp": lax.rem(m + r, mp)}).wait_recv()

    def shares_from(j):
        for i, blk in enumerate(level_blocks(j)):
            k = (j if i == 0 else n - j)
            ref = shares.at[blk, d]
            remote(ref, ref, sz_s.at[k], sz_r.at[k], {"expert": block(k)}).wait_recv()
            share_core(slots[j] + i, blk)

    def norm(place, blk):
        for c in range(dp):
            base = place * pair + c * rows
            lanes = lax.broadcasted_iota(jnp.int32, (rows, shares.shape[3]), 1)
            picked = jnp.where(lanes == e, shares[blk, c], 0.0)
            col[base:base + rows, :] = jnp.sum(picked, axis=1, keepdims=True)

            def chunk(i, _):
                at = pl.ds(pl.multiple_of(i * CHUNK, CHUNK), CHUNK)
                total = jnp.zeros((CHUNK, 1), jnp.float32)
                for q in every:
                    v = x[blk, c, q, at, :].astype(jnp.float32)
                    total = total + jnp.sum(v * v, axis=1, keepdims=True)
                inv = lax.rsqrt(total / full + norm_floor)
                to = pl.ds(pl.multiple_of(base + i * CHUNK, CHUNK), CHUNK)
                for q in every:
                    v = x[blk, c, q, at, :].astype(jnp.float32)
                    normed[to, q * width:(q + 1) * width] = (v * inv * gains[q]).astype(
                        jnp.bfloat16
                    )
                return 0

            lax.fori_loop(0, rows // CHUNK, chunk, 0)

    tile = tile_of(units, 256)
    contract = (((1,), (1,)), ((), ()))

    def hidden(start, blocks):
        for place, blk in enumerate(blocks):
            norm(place, blk)
        size = pair * len(blocks)

        def step(t, _):
            at = pl.ds(pl.multiple_of(t * tile, tile), tile)
            a = normed[0:size, :]
            g = lax.dot_general(a, wg[at, :], contract, preferred_element_type=jnp.float32)
            u = lax.dot_general(a, wu[at, :], contract, preferred_element_type=jnp.float32)
            h = g / (1.0 + jnp.exp(-g)) * u * col[0:size, :]
            hid[start:start + size, at] = h.astype(jnp.bfloat16)
            return 0

        if tile == units:
            a = normed[0:size, :]
            g = lax.dot_general(a, wg[...], contract, preferred_element_type=jnp.float32)
            u = lax.dot_general(a, wu[...], contract, preferred_element_type=jnp.float32)
            h = g / (1.0 + jnp.exp(-g)) * u * col[0:size, :]
            hid[start:start + size, :] = h.astype(jnp.bfloat16)
        else:
            lax.fori_loop(0, units // tile, step, 0)

    from_mp(0, e)
    arrive(1)
    from_core(0, e)
    weights[0].wait()
    weights[1].wait()
    hidden(0, [e])
    for j in range(1, half + 1):
        if j < half:
            arrive(j + 1)
        blocks = level_blocks(j)
        shares_from(j)
        for i, blk in enumerate(blocks):
            from_mp(slots[j] + i, blk)
        for i, blk in enumerate(blocks):
            from_core(slots[j] + i, blk)
        hidden(starts[j], blocks)

    weights[2].wait()
    ctile = tile_of(width, 256)

    def project(start, blocks):
        size = pair * len(blocks)
        for q in every:
            def step(t, _):
                at = pl.ds(pl.multiple_of(t * ctile, ctile), ctile)
                wide = pl.ds(pl.multiple_of(q * width + t * ctile, ctile), ctile)
                y = jnp.dot(hid[start:start + size, :], wd[:, wide],
                            preferred_element_type=jnp.float32).astype(jnp.bfloat16)
                for i, blk in enumerate(blocks):
                    for c in range(dp):
                        base = i * pair + c * rows
                        p[blk, c, q, :, at] = y[base:base + rows]
                return 0

            lax.fori_loop(0, width // ctile, step, 0)

    def add(blk, q, others, begin=0, count=rows):
        def chunk(i, _):
            at = pl.ds(pl.multiple_of(begin + i * CHUNK, CHUNK), CHUNK)
            v = p[blk, d, q, at, :].astype(jnp.float32)
            for ref, index in others:
                v = v + ref[index + (at, slice(None))].astype(jnp.float32)
            p[blk, d, q, at, :] = v.astype(jnp.bfloat16)
            return 0

        lax.fori_loop(0, count // CHUNK, chunk, 0)

    def back_cw(j, blk):
        return remote(piece(p.at[blk, d, m], j, True), piece(rcw.at[j - 1], j, True),
                      rcw_s.at[j], rcw_r.at[j], up_z)

    def back_cc(j, blk):
        return remote(piece(p.at[blk, d, m], j, False), piece(rcc.at[j - 1], j, False),
                      rcc_s.at[j], rcc_r.at[j], down_z)

    def swap(slot, k, blk):
        return remote(p.at[blk, core(k)], rd.at[slot, k - 1], rd_s.at[slot, k], rd_r.at[slot, k],
                      {"dp": core(k)})

    def back_mp(slot, r, blk):
        return remote(p.at[blk, d, part(r)], xr.at[slot, r - 1], xr_s.at[slot, r],
                      xr_r.at[slot, r], {"mp": part(r)})

    def across(j):
        blocks = level_blocks(j)
        project(starts[j], blocks)
        for i, blk in enumerate(blocks):
            for k in range(1, dp):
                send(swap(slots[j] + i, k, blk))
        for i, blk in enumerate(blocks):
            for k in range(1, dp):
                swap(slots[j] + i, k, blk).wait_recv()
            for r in range(1, mp):
                q = part(r)
                add(blk, q, [(rd, (slots[j] + i, k - 1, q)) for k in range(1, dp)])
                send(back_mp(slots[j] + i, r, blk))

    across(half)
    for j in range(half, -1, -1):
        if j > 0:
            across(j - 1)
        blocks = level_blocks(j)
        for i, blk in enumerate(blocks):
            upward = j > 0 and (len(blocks) == 1 or i == 1)
            downward = j > 0 and (len(blocks) == 1 or i == 0)
            others = [(rd, (slots[j] + i, k - 1, m)) for k in range(1, dp)]
            for r in range(1, mp):
                back_mp(slots[j] + i, r, blk).wait_recv()
                others.append((xr, (slots[j] + i, r - 1)))
            add(blk, m, others)
            if j < half and (upward or j == 0):
                back_cw(j + 1, blk).wait_recv()
                split = 2 * (j + 1) == n
                add(blk, m, [(rcw, (j,))], 0, rows // 2 if split else rows)
            if j < half and (downward or j == 0):
                back_cc(j + 1, blk).wait_recv()
                split = 2 * (j + 1) == n
                add(blk, m, [(rcc, (j,))], rows // 2 if split else 0,
                    rows // 2 if split else rows)
            if upward:
                send(back_cw(j, blk))
            if downward:
                send(back_cc(j, blk))

    def last(i, _):
        at = pl.ds(pl.multiple_of(i * CHUNK, CHUNK), CHUNK)
        v = p[e, d, m, at, :].astype(jnp.float32)
        out_ref[at, :] = (cur_ref[at, :].astype(jnp.float32) + v).astype(jnp.bfloat16)
        return 0

    lax.fori_loop(0, rows // CHUNK, last, 0)
    for copy in sent:
        copy.wait_send()


def layer(layer_idx, n, dp, mp, current, gain, share, w_gate, w_up, w_down):
    rows, width = current.shape
    units, full = w_gate.shape[2:]
    half = n // 2
    bf, dma = jnp.bfloat16, pltpu.SemaphoreType.DMA
    vmem = pl.BlockSpec(memory_space=pltpu.VMEM)
    hbm = pl.BlockSpec(memory_space=pl.ANY)
    return pl.pallas_call(
        functools.partial(layer_kernel, layer_idx, n, dp, mp),
        out_shape=jax.ShapeDtypeStruct((rows, width), bf),
        in_specs=[vmem, vmem, vmem, hbm, hbm, hbm],
        out_specs=vmem,
        scratch_shapes=[
            pltpu.VMEM((units, full), bf),
            pltpu.VMEM((units, full), bf),
            pltpu.VMEM((units, full), bf),
            pltpu.VMEM((n, dp, mp, rows, width), bf),
            pltpu.VMEM((n, dp, mp, rows, width), bf),
            pltpu.VMEM((n, max(dp - 1, 1), mp, rows, width), bf),
            pltpu.VMEM((half, rows, width), bf),
            pltpu.VMEM((half, rows, width), bf),
            pltpu.VMEM((n, max(mp - 1, 1), rows, width), bf),
            pltpu.VMEM((2 * dp * rows, full), bf),
            pltpu.VMEM((n * dp * rows, units), bf),
            pltpu.VMEM((2 * dp * rows, 1), jnp.float32),
            pltpu.VMEM((mp, 1, width), jnp.float32),
            pltpu.VMEM((n, dp, rows, share.shape[1]), jnp.float32),
            dma((3,)), dma((3,)), dma((n, mp)), dma((n, mp)),
            dma((half + 1,)), dma((half + 1,)), dma((half + 1,)), dma((half + 1,)),
            dma((n, mp, dp)), dma((n, mp, dp)),
            dma((n, dp)), dma((n, dp)), dma((n,)), dma((n,)), dma((mp,)), dma((mp,)),
            dma((n, dp)), dma((n, dp)),
            dma((half + 1,)), dma((half + 1,)), dma((half + 1,)), dma((half + 1,)),
            dma((n, mp)), dma((n, mp)),
        ],
        compiler_params=pltpu.CompilerParams(
            collective_id=layer_idx, has_side_effects=True, vmem_limit_bytes=67043328
        ),
    )(current, gain, share, w_gate, w_up, w_down)


def body(hidden_in, norm_gain, expert_ids, gate_counts, exit_layer, w_gate, w_up, w_down):
    n, dp, mp = lax.axis_size("expert"), lax.axis_size("dp"), lax.axis_size("mp")
    rows, width = hidden_in.shape
    expert_range = jnp.arange(n, dtype=jnp.int32)
    counts = gate_counts.astype(jnp.float32)
    gate_share = counts / jnp.sum(counts, axis=2, keepdims=True)
    active = exit_layer[None, :] > jnp.arange(LAYERS, dtype=jnp.int32)[:, None]
    matched = (expert_ids[..., None] == expert_range) & active[:, :, None, None]
    share = jnp.sum(jnp.where(matched, gate_share[..., None], jnp.float32(0.0)), axis=2)
    share = jnp.pad(share, ((0, 0), (0, 0), (0, -n % 128)))
    gain = norm_gain.astype(jnp.float32)[:, None, :]
    current = hidden_in
    for layer_idx in range(LAYERS):
        current = layer(
            layer_idx, n, dp, mp, current, gain[layer_idx], share[layer_idx], w_gate, w_up, w_down
        )
    return current


def solution(mesh):
    in_specs = (
        P(("groups", "expert", "dp"), "mp"),
        P(None, "mp"),
        P(None, ("groups", "expert", "dp"), None),
        P(None, ("groups", "expert", "dp"), None),
        P(("groups", "expert", "dp")),
        P(None, "expert", ("mp", "dp"), None),
        P(None, "expert", ("mp", "dp"), None),
        P(None, "expert", ("mp", "dp"), None),
    )
    out_specs = P(("groups", "expert", "dp"), "mp")
    return jax.shard_map(body, mesh=mesh, in_specs=in_specs, out_specs=out_specs, check_vma=False)
```

time: 227 us -> 205 us (0.903)
  blocking collectives: 21.1 us -> 0 us
    all_gather x2 -> x0, blocking collectives: 21.1 us -> none  [the longest x1 16.5 us: body(): share = lax.all_gather(share, ('expert', 'dp'), axis=1, tiled=True)]
where the time goes in v3:
time: 205 us
  Pallas kernels  199 us (97%)
  local copies, waits for them, and re-layouts  3.8 us (2%)
  other arithmetic  2.13 us (1%)
    pallas_call x2, Pallas kernels, layer(): pl.pallas_call(functools.partial(layer_kernel, layer_idx, n, dp, mp), out...  199 us

profile of v3, /device:TPU:0, one launch (start us, length us, event | category | flops | bytes accessed | tf_op | source)
XLA Modules:
  0.0 204.9 jit_solution(9136854364386584722)
XLA Ops:
  0.0 0.7 iota_compare_fusion.1
  0.7 0.8 convert_divide_fusion
  1.4 0.7 select_reduce_fusion
  2.1 1.4 fusion.8
  3.5 0.1 copy.11
  3.6 0.6 fusion.1
  4.3 101.1 %shard_map.82.cur_ref = bf16[64,2048]{1,0:T(8,128)(2,1)} custom-call(bf16[64,2048]{1,0:T(8,128)(2,1)} %cur_ref.1, f32[1,2048]{1,0:T(1,128)} %get-tuple-element.8.gain_ref, f32[64,128]{1,0:T(8,128)} %get-tuple-element.6.share_ref, bf16[2,1,1792,4096]{3,2,1,0:T(8,128)(2,1)} %wg_hbm.3, bf16[2,1,1792,4096]{3,2,1,0:T(8,128)(2,1)} %wu_hbm.3, ...), custom_call_target="tpu_custom_call" | custom-call | tf_op jit(solution)/shard_map/pallas_call | solution.py:355
  105.4 97.9 %shard_map.83 = bf16[64,2048]{1,0:T(8,128)(2,1)} custom-call(bf16[64,2048]{1,0:T(8,128)(2,1)} %shard_map.82.cur_ref, f32[1,2048]{1,0:T(1,128)} %get-tuple-element.7.gain_ref, f32[64,128]{1,0:T(8,128)} %get-tuple-element.5.share_ref, bf16[2,1,1792,4096]{3,2,1,0:T(8,128)(2,1)} %wg_hbm.3, bf16[2,1,1792,4096]{3,2,1,0:T(8,128)(2,1)} %wu_hbm.3, ...), custom_call_target="tpu_custom_call" | custom-call | tf_op jit(solution)/shard_map/pallas_call | solution.py:355
  203.3 1.7 copy.13
